TPU v7x, 32 devices: a whole 2x2x4 slice. The times are simulated.
32 devices in a mesh: data: 2 (over x), expert: 16 (over z, y, core).
Axes of the slice: x: 2, y: 2, z: 4, core: 2. Of those that a mesh axis runs over, the one named last changes fastest.
Arguments:
- x: bfloat16 [2048, 2048], P(('data', 'expert')), parts along dimension 0
- idx: int32 [2048, 8], P(('data', 'expert')), parts along dimension 0
- g: float32 [2048, 8], P(('data', 'expert')), parts along dimension 0
- hot_tok: int32 [1024], P(('data', 'expert')), parts along dimension 0
- W1: bfloat16 [64, 2048, 1024], P('expert')
- W3: bfloat16 [64, 2048, 1024], P('expert')
- W2: bfloat16 [64, 1024, 2048], P('expert')
Outputs:
- output: bfloat16 [2048, 2048], P(('data', 'expert')), parts along dimension 0
There are 2 independent parts. A program takes and returns all parts, laid end to end along the dimension named above; an argument that names none is the same for every part.
All inputs are finite; a program needn't handle non-finite values.
Results may differ from a plain program's by a relative error of at most 0.001.
Values are sent between devices in bfloat16 or wider.
A program may use at most 1 GiB of HBM per device.

v0:
```python
import jax
import jax.numpy as jnp
from jax import lax
from jax.sharding import PartitionSpec as P


def _dest(idx, hot_tok, n, el, ch, cap):
    t, k = idx.shape
    s = ch + (el - 1) * cap
    flat = idx.reshape(-1)
    onehot = (flat[:, None] == jnp.arange(n * el, dtype=jnp.int32)[None, :]).astype(jnp.int32)
    rank = jnp.take_along_axis(jnp.cumsum(onehot, axis=0) - onehot, flat[:, None], axis=1).reshape(t, k)
    hot_rank = jnp.zeros((t,), jnp.int32).at[hot_tok].set(jnp.arange(ch, dtype=jnp.int32))
    loc = idx % el
    pos = (idx // el) * s + jnp.where(loc == 0, rank, ch + (loc - 1) * cap + rank)
    return jnp.where(idx == 0, hot_rank[:, None], pos)


def _send(x, dest, rows):
    t, d = x.shape
    k = dest.shape[1]
    src = jnp.full((rows,), t, jnp.int32).at[dest.reshape(-1)].set(jnp.repeat(jnp.arange(t, dtype=jnp.int32), k))
    return jnp.concatenate([x, jnp.zeros((1, d), x.dtype)])[src]


def _combine(back, dest, g):
    y = jnp.zeros((dest.shape[0], back.shape[1]), jnp.float32)
    for j in range(dest.shape[1]):
        y = y + g[:, j:j + 1] * back[dest[:, j]].astype(jnp.float32)
    return y.astype(jnp.bfloat16)


def _experts(xs, w1, w3, w2, form_in, form_out):
    a = jnp.einsum(form_in, xs, w1, preferred_element_type=jnp.float32)
    b = jnp.einsum(form_in, xs, w3, preferred_element_type=jnp.float32)
    u = (jax.nn.silu(a) * b).astype(jnp.bfloat16)
    return jnp.einsum(form_out, u, w2, preferred_element_type=jnp.float32).astype(jnp.bfloat16)


def solution(mesh):
    n = mesh.shape['expert']

    def local(x, idx, g, hot_tok, w1, w3, w2):
        t, d = x.shape
        k = idx.shape[1]
        el = w1.shape[0]
        e = el * n
        ch = hot_tok.shape[0]
        cap = 2 * ((t * k - ch + e - 2) // (e - 1))
        s = ch + (el - 1) * cap
        dest = _dest(idx, hot_tok, n, el, ch, cap)
        send = _send(x, dest, n * s).reshape(n, s, d)
        recv = lax.all_to_all(send, 'expert', 0, 0, tiled=True)
        out = _experts(recv[:, :ch], w1[0], w3[0], w2[0], 'rcd,df->rcf', 'rcf,fd->rcd')
        if el > 1:
            xc = recv[:, ch:].reshape(n, el - 1, cap, d)
            oc = _experts(xc, w1[1:], w3[1:], w2[1:], 'recd,edf->recf', 'recf,efd->recd')
            out = jnp.concatenate([out, oc.reshape(n, (el - 1) * cap, d)], axis=1)
        back = lax.all_to_all(out, 'expert', 0, 0, tiled=True)
        return _combine(back.reshape(n * s, d), dest, g)

    rows = P(('data', 'expert'))
    wspec = P('expert')
    return jax.shard_map(local, mesh=mesh, in_specs=(rows, rows, rows, rows, wspec, wspec, wspec), out_specs=rows, check_vma=False)
```

profile of v0, /device:TPU:13, one launch (start us, length us, event | category | flops | bytes accessed | tf_op | source)
XLA Modules:
  0.0 341.8 jit_solution(13578092370636404211)
XLA Ops:
  0.0 0.8 copy.40
  1.9 1.2 reduce-window.6
  3.5 4.5 %gather_fusion.9 = s32[512]{0:T(512)S(1)} fusion(s32[512,64]{0,1:T(8,128)S(1)} %fusion.48, s32[512]{0:T(512)S(1)} %bitcast.112), kind=kCustom, calls=%fused_computation.9 | custom fusion | bytes 8192 | tf_op jit(solution)/shard_map/jit(take_along_axis)/gather | solution.py:12
  9.8 2.5 scatter_custom_fusion.1
  12.2 1.0 concatenate.6
  13.2 6.1 %gather_fusion = bf16[1280,2048]{1,0:T(8,128)(2,1)} fusion(bf16[65,2048]{1,0:T(8,128)(2,1)S(1)} %concatenate.6, s32[2048]{0:T(1024)S(1)} %pad_clamp_fusion), kind=kCustom, calls=%fused_computation | custom fusion | bytes 10490880 | tf_op jit(solution)/shard_map/gather | solution.py:23
  19.3 120.9 %all_to_all.10 = bf16[16,80,2048]{2,1,0:T(8,128)(2,1)S(1)} all-to-all(bf16[16,80,2048]{2,1,0:T(8,128)(2,1)} %bitcast.113), channel_id=1, replica_groups=mesh['data'=2,'expert'=16] {'expert'}, dimensions={0} | all-to-all | bytes 10485760 | tf_op jit(solution)/shard_map/all_to_all | solution.py:53
  140.7 8.0 %fusion.2 = f32[3,16,16,1024]{3,2,1,0:T(8,128)S(1)} fusion(bf16[4,2048,1024]{2,1,0:T(8,128)(2,1)} %param.12, bf16[16,3,16,2048]{3,2,1,0:T(8,128)(2,1)S(1)} %bitcast.115), kind=kOutput, calls=%fused_computation.14 | convolution fusion | flops 3221225472 | bytes 18874368 | tf_op jit(solution)/shard_map/recd,edf->recf/dot_general | solution.py:35
  148.7 8.2 %fusion.21 = bf16[16,3,16,1024]{3,2,0,1:T(8,128)(2,1)S(1)} fusion(f32[3,16,16,1024]{3,2,1,0:T(8,128)S(1)} %fusion.2, bf16[4,2048,1024]{2,1,0:T(8,128)(2,1)} %param.11, bf16[16,3,16,2048]{3,2,1,0:T(8,128)(2,1)S(1)} %bitcast.116), kind=kOutput, calls=%fused_computation.33 | convolution fusion | flops 3225944064 | bytes 20447232 | tf_op jit(solution)/shard_map/recd,edf->recf/dot_general | solution.py:34
  157.0 8.0 %fusion.25 = bf16[16,3,16,2048]{3,2,0,1:T(8,128)(2,1)S(1)} fusion(bf16[16,3,16,1024]{3,2,0,1:T(8,128)(2,1)S(1)} %fusion.21, bf16[4,1024,2048]{2,1,0:T(8,128)(2,1)} %param.13), kind=kOutput, calls=%fused_computation.39 | convolution fusion | flops 3222798336 | bytes 17301504 | tf_op jit(solution)/shard_map/recf,efd->recd/dot_general | solution.py:37
  165.4 5.9 %fusion.11 = f32[16,32,1024]{2,1,0:T(8,128)} fusion(bf16[4,2048,1024]{2,1,0:T(8,128)(2,1)} %param.12, bf16[16,80,2048]{2,1,0:T(8,128)(2,1)S(1)} %all_to_all.10), kind=kOutput, calls=%fused_computation.24 | convolution fusion | flops 2147483648 | bytes 8388608 | tf_op jit(solution)/shard_map/rcd,df->rcf/dot_general | solution.py:35
  171.3 10.7 %fusion.28 = bf16[16,32,2048]{2,1,0:T(8,128)(2,1)} fusion(bf16[4,1024,2048]{2,1,0:T(8,128)(2,1)} %param.13, f32[16,32,1024]{2,1,0:T(8,128)} %fusion.11, bf16[4,2048,1024]{2,1,0:T(8,128)(2,1)} %param.11, bf16[16,80,2048]{2,1,0:T(8,128)(2,1)} %copy-done), kind=kOutput, calls=%fused_computation.40 | convolution fusion | flops 4299161600 | bytes 14680064 | tf_op jit(solution)/shard_map/rcf,fd->rcd/dot_general | solution.py:37
  182.0 4.6 %pad_maximum_fusion = bf16[16,80,2048]{2,1,0:T(8,128)(2,1)} fusion(bf16[16,48,2048]{2,1,0:T(8,128)(2,1)S(1)} %bitcast.114, bf16[16,32,2048]{2,1,0:T(8,128)(2,1)} %fusion.28), kind=kLoop, calls=%fused_computation.21 | loop fusion | flops 10485760 | bytes 10485760 | tf_op jit(solution)/shard_map/concatenate | solution.py:58
  186.6 5.6 %all-to-all-start.1 = ((bf16[16,80,2048]{2,1,0:T(8,128)(2,1)}), bf16[16,80,2048]{2,1,0:T(8,128)(2,1)}, u32[]{:S(2)}, u32[]{:S(2)}) async-start(bf16[16,80,2048]{2,1,0:T(8,128)(2,1)} %pad_maximum_fusion), calls=%async_computation.1 | async-start | bytes 10485760 | tf_op jit(solution)/shard_map/all_to_all | solution.py:59
  192.3 115.1 %all-to-all-done.1 = bf16[16,80,2048]{2,1,0:T(8,128)(2,1)} async-done(((bf16[16,80,2048]{2,1,0:T(8,128)(2,1)}), bf16[16,80,2048]{2,1,0:T(8,128)(2,1)}, u32[]{:S(2)}, u32[]{:S(2)}) %all-to-all-start.1) | async-done | bytes 5242912 | tf_op jit(solution)/shard_map/all_to_all | solution.py:59
  307.4 4.1 %gather_fusion.8 = bf16[64,2048]{1,0:T(8,128)(2,1)S(1)} fusion(bf16[1280,2048]{1,0:T(8,128)(2,1)} %bitcast.23, s32[1024]{0:T(1024)S(1)} %get-tuple-element.21), kind=kCustom, calls=%fused_computation.8 | custom fusion | bytes 524544 | tf_op jit(solution)/shard_map/gather | solution.py:29
  311.5 4.1 %gather_fusion.7 = bf16[64,2048]{1,0:T(8,128)(2,1)S(1)} fusion(bf16[1280,2048]{1,0:T(8,128)(2,1)} %bitcast.23, s32[1024]{0:T(1024)S(1)} %get-tuple-element.22), kind=kCustom, calls=%fused_computation.7 | custom fusion | bytes 524544 | tf_op jit(solution)/shard_map/gather | solution.py:29
  315.7 4.1 %gather_fusion.6 = bf16[64,2048]{1,0:T(8,128)(2,1)S(1)} fusion(bf16[1280,2048]{1,0:T(8,128)(2,1)} %bitcast.23, s32[1024]{0:T(1024)S(1)} %get-tuple-element.23), kind=kCustom, calls=%fused_computation.6 | custom fusion | bytes 524544 | tf_op jit(solution)/shard_map/gather | solution.py:29
  319.8 4.1 %gather_fusion.5 = bf16[64,2048]{1,0:T(8,128)(2,1)S(1)} fusion(bf16[1280,2048]{1,0:T(8,128)(2,1)} %bitcast.23, s32[1024]{0:T(1024)S(1)} %get-tuple-element.24), kind=kCustom, calls=%fused_computation.5 | custom fusion | bytes 524544 | tf_op jit(solution)/shard_map/gather | solution.py:29
  324.0 4.1 %gather_fusion.4 = bf16[64,2048]{1,0:T(8,128)(2,1)S(1)} fusion(bf16[1280,2048]{1,0:T(8,128)(2,1)} %bitcast.23, s32[1024]{0:T(1024)S(1)} %get-tuple-element.25), kind=kCustom, calls=%fused_computation.4 | custom fusion | bytes 524544 | tf_op jit(solution)/shard_map/gather | solution.py:29
  328.1 4.1 %gather_fusion.3 = bf16[64,2048]{1,0:T(8,128)(2,1)S(1)} fusion(bf16[1280,2048]{1,0:T(8,128)(2,1)} %bitcast.23, s32[1024]{0:T(1024)S(1)} %get-tuple-element.26), kind=kCustom, calls=%fused_computation.3 | custom fusion | bytes 524544 | tf_op jit(solution)/shard_map/gather | solution.py:29
  332.3 4.1 %gather_fusion.2 = bf16[64,2048]{1,0:T(8,128)(2,1)S(1)} fusion(bf16[1280,2048]{1,0:T(8,128)(2,1)} %bitcast.23, s32[1024]{0:T(1024)S(1)} %get-tuple-element.27), kind=kCustom, calls=%fused_computation.2 | custom fusion | bytes 524544 | tf_op jit(solution)/shard_map/gather | solution.py:29
  336.4 4.1 %gather_fusion.1 = bf16[64,2048]{1,0:T(8,128)(2,1)S(1)} fusion(bf16[1280,2048]{1,0:T(8,128)(2,1)} %bitcast.23, s32[1024]{0:T(1024)S(1)} %get-tuple-element.28), kind=kCustom, calls=%fused_computation.1 | custom fusion | bytes 524544 | tf_op jit(solution)/shard_map/gather | solution.py:29
  340.6 1.2 add_convert_fusion
  (37 shorter events, 4.0 us)
Async XLA Ops:
  140.2 25.1 %copy-start = (bf16[16,80,2048]{2,1,0:T(8,128)(2,1)}, bf16[16,80,2048]{2,1,0:T(8,128)(2,1)S(1)}, u32[]{:S(2)}) copy-start(bf16[16,80,2048]{2,1,0:T(8,128)(2,1)S(1)} %all_to_all.10) | copy-start | bytes 15728644
  186.6 5.7 %copy-start.1 = (f32[64,8]{0,1:T(8,128)S(1)}, f32[64,8]{0,1:T(8,128)}, u32[]{:S(2)}) copy-start(f32[64,8]{0,1:T(8,128)} %param.9) | copy-start | bytes 6148
  186.6 120.8 %all-to-all-start.1 = ((bf16[16,80,2048]{2,1,0:T(8,128)(2,1)}), bf16[16,80,2048]{2,1,0:T(8,128)(2,1)}, u32[]{:S(2)}, u32[]{:S(2)}) async-start(bf16[16,80,2048]{2,1,0:T(8,128)(2,1)} %pad_maximum_fusion), calls=%async_computation.1 | async-start | bytes 10485760 | tf_op jit(solution)/shard_map/all_to_all | solution.py:59
where the time goes:
time: 343 us; the launch traced here: 342 us
  blocking collectives  121 us (35%)
  waiting for transfers between devices  115 us (34%)
  local copies, waits for them, and re-layouts  50.4 us (15%)
  matrix products  40.9 us (12%)
  other arithmetic  8.56 us (2%)
  starting transfers between devices  5.64 us (2%)
    all_to_all x1, blocking collectives, local(): recv = lax.all_to_all(send, 'expert', 0, 0, tiled=True)  121 us
    all_to_all x1, waiting for transfers between devices, local(): back = lax.all_to_all(out, 'expert', 0, 0, tiled=True)  115 us
    gather x8, local copies, waits for them, and re-layouts, _combine(): y = y + g[:, j:j + 1] * back[dest[:, j]].astype(jnp.float32)  33.2 us
    dot_general x2, matrix products, _experts(): jnp.einsum(form_out, u, w2, preferred_element_type=jnp.float32)  18.7 us
    dot_general x2, matrix products, _experts(): b = jnp.einsum(form_in, xs, w3, preferred_element_type=jnp.float32)  13.9 us
    dot_general x1, matrix products, _experts(): a = jnp.einsum(form_in, xs, w1, preferred_element_type=jnp.float32)  8.25 us
  transfers between devices with their start and end apart: 1, of which 1 were waited for; matrix products, arithmetic and copies ran while one was open for 0% of the time, Pallas kernels for 0%

commit v1 on v0

v1 whole, which is shorter than its diff:
```python
import jax
import jax.numpy as jnp
from jax import lax
from jax.sharding import PartitionSpec as P


def _pieces(g):
    hi = lax.reduce_precision(g, 8, 7)
    mid = lax.reduce_precision(g - hi, 8, 7)
    lo = g - hi - mid
    return hi.astype(jnp.bfloat16), mid.astype(jnp.bfloat16), lo.astype(jnp.bfloat16)


def _expert(xs, w1, w3, w2):
    a = jnp.dot(xs, w1, preferred_element_type=jnp.float32)
    b = jnp.dot(xs, w3, preferred_element_type=jnp.float32)
    u = (jax.nn.silu(a) * b).astype(jnp.bfloat16)
    return jnp.dot(u, w2, preferred_element_type=jnp.float32).astype(jnp.bfloat16)


def solution(mesh):
    n = mesh.shape['expert']

    def local(x, idx, g, hot_tok, w1, w3, w2):
        t, d = x.shape
        k = idx.shape[1]
        el = w1.shape[0]
        e = el * n
        ch = hot_tok.shape[0]
        cap = 2 * ((t * k - ch + e - 2) // (e - 1))
        me = lax.axis_index('expert')
        meta = jnp.concatenate([idx.astype(jnp.float32).T, g.T], axis=0)
        meta = lax.all_gather(meta, 'expert', axis=0)
        xall = lax.all_gather(x, 'expert', axis=0)
        ids, gs = meta[:, :k], meta[:, k:]
        mine = (me * el + jnp.arange(el)).astype(jnp.float32)
        eq = ids[:, None] == mine[None, :, None, None]
        gate = jnp.where(eq, gs[:, None], 0.0).sum(axis=2)
        hit = eq.any(axis=2)
        tri = (jnp.arange(t)[:, None] < jnp.arange(t)[None, :]).astype(jnp.bfloat16)
        rank = jnp.dot(hit.astype(jnp.bfloat16), tri, preferred_element_type=jnp.float32)
        rank = jnp.where(hit, rank, -1.0)
        sizes = [ch] + [cap] * (el - 1)
        offs = [sum(sizes[:i]) for i in range(el)]
        oh = jnp.concatenate([rank[:, i, None, :] == jnp.arange(sizes[i], dtype=jnp.float32)[None, :, None] for i in range(el)], axis=1)
        gg = jnp.concatenate([jnp.broadcast_to(gate[:, i, None, :], (n, sizes[i], t)) for i in range(el)], axis=1)
        gg = jnp.where(oh, gg, 0.0)
        xs = jnp.einsum('nst,ntd->nsd', oh.astype(jnp.bfloat16), xall, preferred_element_type=jnp.float32).astype(jnp.bfloat16)
        hs = []
        for i in range(el):
            xe = xs[:, offs[i]:offs[i] + sizes[i]].reshape(n * sizes[i], d)
            hs.append(_expert(xe, w1[i], w3[i], w2[i]).reshape(n, sizes[i], d))
        h = jnp.concatenate(hs, axis=1)
        g3 = jnp.concatenate(_pieces(gg), axis=1)
        h3 = jnp.concatenate([h, h, h], axis=1)
        part = jnp.einsum('nst,nsd->ntd', g3, h3, preferred_element_type=jnp.float32)
        y = lax.psum_scatter(part.reshape(n * t, d), 'expert', scatter_dimension=0, tiled=True)
        return y.astype(jnp.bfloat16)

    rows = P(('data', 'expert'))
    wspec = P('expert')
    return jax.shard_map(local, mesh=mesh, in_specs=(rows, rows, rows, rows, wspec, wspec, wspec), out_specs=rows, check_vma=False)
```

time: 343 us -> 240 us (0.70)
  the two profiles are of different devices: /device:TPU:13 before, /device:TPU:0 now
where the time goes in v1:
time: 240 us
  waiting for transfers between devices  129 us (54%)
  matrix products  56.3 us (23%)
  blocking collectives  23.7 us (10%)
  between operations  13.6 us (6%)
  local copies, waits for them, and re-layouts  10.9 us (5%)
  other arithmetic  6.18 us (3%)
    reduce_scatter x1, waiting for transfers between devices, local(): lax.psum_scatter(part.reshape(n * t, d), 'expert', scatter_dimension=0, t...  102 us
    dot_general x4, matrix products, _expert(): jnp.dot(u, w2, preferred_element_type=jnp.float32).astype(jnp.bfloat16)  31 us
    all_gather x1, waiting for transfers between devices, local(): xall = lax.all_gather(x, 'expert', axis=0)  26.4 us
    all_gather x1, blocking collectives, local(): meta = lax.all_gather(meta, 'expert', axis=0)  23.7 us
    dot_general x4, matrix products, _expert(): a = jnp.dot(xs, w1, preferred_element_type=jnp.float32)  15.1 us
    unnamed x27, local copies, waits for them, and re-layouts  8.55 us
    dot_general x1, matrix products, local(): jnp.einsum('nst,nsd->ntd', g3, h3, preferred_element_type=jnp.float32)  6.17 us
  transfers between devices with their start and end apart: 2, of which 2 were waited for; matrix products, arithmetic and copies ran while one was open for 2% of the time, Pallas kernels for 0%

profile of v1, /device:TPU:0, one launch (start us, length us, event | category | flops | bytes accessed | tf_op | source)
XLA Modules:
  0.0 240.1 jit_solution(2437352897208063960)
XLA Ops:
  6.5 0.7 all-gather.4.cloned.1.call-update
  7.3 0.7 convert_bitcast_fusion
  8.0 0.7 pad_maximum_fusion
  8.7 23.7 %all-gather = f32[256,64]{1,0:T(8,128)S(1)} all-gather(f32[16,64]{1,0:T(8,128)S(1)} %pad_maximum_fusion), channel_id=2, replica_groups=mesh['data'=2,'expert'=16] {'expert'}, dimensions={0}, use_global_device_ids=true | all-gather | bytes 69632 | tf_op jit(solution)/shard_map/all_gather | solution.py:33
  34.5 0.7 reduce-precision_convert_fusion.1
  35.2 1.2 reduce-precision_convert_fusion
  36.4 26.4 %all-gather.4.cloned.1.call-done = bf16[1024,2048]{1,0:T(8,128)(2,1)} async-done(((bf16[64,2048]{1,0:T(8,128)(2,1)}), bf16[1024,2048]{1,0:T(8,128)(2,1)}) %all-gather.4.cloned.1.call-update) | async-done | bytes 4194320 | tf_op jit(solution)/shard_map/all_gather | solution.py:34
  62.8 3.9 %convolution_convert_fusion = bf16[16,80,2048]{2,1,0:T(8,128)(2,1)S(1)} fusion(pred[16,80,64]{1,2,0:T(32,128)(4,1)S(1)} %get-tuple-element.6, bf16[16,64,2048]{2,1,0:T(8,128)(2,1)} %bitcast.119), kind=kOutput, calls=%fused_computation.36 | convolution fusion | flops 338165760 | bytes 9519104 | tf_op jit(solution)/shard_map/nst,ntd->nsd/dot_general | solution.py:48
  66.9 1.2 fusion.95
  68.1 3.6 %copy-done.7 = bf16[4,2048,1024]{2,1,0:T(8,128)(2,1)S(1)} copy-done((bf16[4,2048,1024]{2,1,0:T(8,128)(2,1)S(1)}, bf16[4,2048,1024]{2,1,0:T(8,128)(2,1)}, u32[]{:S(2)}) %copy-start.7) | copy-done | bytes 16777240
  71.7 2.3 fusion.10
  74.0 2.3 fusion.4
  76.2 6.5 %fusion.42 = bf16[256,2048]{1,0:T(8,128)(2,1)S(1)} fusion(bf16[4,1024,2048]{2,1,0:T(8,128)(2,1)} %param.12, bf16[256,2048]{1,0:T(8,128)(2,1)} %bitcast.127, bf16[4,2048,1024]{2,1,0:T(8,128)(2,1)} %param.11, f32[256,1024]{1,0:T(8,128)} %fusion.10), kind=kOutput, calls=%fused_computation.39 | convolution fusion | flops 2149580800 | bytes 11534336 | tf_op jit(solution)/shard_map/dot_general | solution.py:18
  82.8 7.5 %fusion.45 = bf16[256,2048]{1,0:T(8,128)(2,1)} fusion(bf16[4,1024,2048]{2,1,0:T(8,128)(2,1)} %param.12, bf16[256,2048]{1,0:T(8,128)(2,1)} %bitcast.125, bf16[4,2048,1024]{2,1,0:T(8,128)(2,1)} %param.11, f32[256,1024]{1,0:T(8,128)} %fusion.4), kind=kOutput, calls=%fused_computation.40 | convolution fusion | flops 2149580800 | bytes 11534336 | tf_op jit(solution)/shard_map/dot_general | solution.py:18
  90.3 4.8 %fusion.16 = f32[256,1024]{1,0:T(8,128)} fusion(bf16[256,2048]{1,0:T(8,128)(2,1)} %bitcast.122, bf16[4,2048,1024]{2,1,0:T(8,128)(2,1)} %param.10), kind=kOutput, calls=%fused_computation.16 | convolution fusion | flops 1073741824 | bytes 6291456 | tf_op jit(solution)/shard_map/dot_general | solution.py:15
  95.0 7.7 %fusion.39 = bf16[256,2048]{1,0:T(8,128)(2,1)} fusion(bf16[4,1024,2048]{2,1,0:T(8,128)(2,1)} %param.12, bf16[256,2048]{1,0:T(8,128)(2,1)} %bitcast.123, bf16[4,2048,1024]{2,1,0:T(8,128)(2,1)} %param.11, f32[256,1024]{1,0:T(8,128)} %fusion.16), kind=kOutput, calls=%fused_computation.38 | convolution fusion | flops 2149580800 | bytes 11534336 | tf_op jit(solution)/shard_map/dot_general | solution.py:18
  102.8 5.8 %fusion.22 = f32[512,1024]{1,0:T(8,128)} fusion(bf16[512,2048]{1,0:T(8,128)(2,1)S(1)} %bitcast.120, bf16[4,2048,1024]{2,1,0:T(8,128)(2,1)} %param.10), kind=kOutput, calls=%fused_computation.22 | convolution fusion | flops 2147483648 | bytes 8388608 | tf_op jit(solution)/shard_map/dot_general | solution.py:15
  108.6 9.2 %fusion.36 = bf16[512,2048]{1,0:T(8,128)(2,1)S(1)} fusion(bf16[4,1024,2048]{2,1,0:T(8,128)(2,1)} %param.12, f32[512,1024]{1,0:T(8,128)} %fusion.22, bf16[512,2048]{1,0:T(8,128)(2,1)} %bitcast.121, bf16[4,2048,1024]{2,1,0:T(8,128)(2,1)} %param.11), kind=kOutput, calls=%fused_computation.37 | convolution fusion | flops 4299161600 | bytes 14680064 | tf_op jit(solution)/shard_map/dot_general | solution.py:18
  118.0 1.5 constant_dynamic-update-slice_fusion.10
  119.6 1.3 constant_dynamic-update-slice_fusion.8
  121.1 1.3 constant_dynamic-update-slice_fusion.6
  123.1 6.2 %fusion.77 = f32[16,64,2048]{2,1,0:T(8,128)} fusion(bf16[16,240,2048]{2,1,0:T(8,128)(2,1)S(1)} %constant_dynamic-update-slice_fusion, bf16[16,80,64]{1,2,0:T(8,128)(2,1)S(1)} %copy-done.4, bf16[16,80,64]{1,2,0:T(8,128)(2,1)S(1)} %copy-done.3, bf16[16,80,64]{1,2,0:T(8,128)(2,1)S(1)} %get-tuple-element.5), kind=kOutput, calls=%fused_computation.55 | convolution fusion | flops 1008107520 | bytes 24608768 | tf_op jit(solution)/shard_map/nst,nsd->ntd/dot_general | solution.py:56
  129.3 102.2 %reduce-scatter.2.cloned.1.call-done = f32[64,2048]{1,0:T(8,128)} async-done(((f32[1024,2048]{1,0:T(8,128)}), f32[64,2048]{1,0:T(8,128)}) %reduce-scatter.2.cloned.1.call-update) | async-done | bytes 524304 | tf_op jit(solution)/shard_map/reduce_scatter | solution.py:57
  231.5 1.8 convert_element_type.66
  (42 shorter events, 3.2 us)
Async XLA Ops:
  6.5 56.3 %all-gather.4.cloned.1.call-start = ((), (), s32[]{:S(2)}) async-start(), calls=%async_computation.2 | async-start | bytes 4456448 | tf_op jit(solution)/shard_map/all_gather | solution.py:34
  7.3 224.2 %reduce-scatter.2.cloned.1.call-start = ((), (), s32[]{:S(2)}) async-start(), calls=%async_computation.1 | async-start | bytes 8912896 | tf_op jit(solution)/shard_map/reduce_scatter | solution.py:57
  62.8 8.9 %copy-start.7 = (bf16[4,2048,1024]{2,1,0:T(8,128)(2,1)S(1)}, bf16[4,2048,1024]{2,1,0:T(8,128)(2,1)}, u32[]{:S(2)}) copy-start(bf16[4,2048,1024]{2,1,0:T(8,128)(2,1)} %param.10) | copy-start | bytes 50331652
  66.9 35.9 %copy-start.2 = (bf16[16,32,2048]{2,1,0:T(8,128)(2,1)}, bf16[16,32,2048]{2,1,0:T(8,128)(2,1)S(1)}, u32[]{:S(2)}) copy-start(bf16[16,32,2048]{2,1,0:T(8,128)(2,1)S(1)} %slice.114) | copy-start | bytes 6291460
  68.1 5.8 %copy-start.5 = (bf16[16,16,2048]{2,1,0:T(8,128)(2,1)}, bf16[16,16,2048]{2,1,0:T(8,128)(2,1)S(1)}, u32[]{:S(2)}) copy-start(bf16[16,16,2048]{2,1,0:T(8,128)(2,1)S(1)} %get-tuple-element.7) | copy-start | bytes 3145732
  68.1 5.9 %copy-start.6 = (bf16[16,16,2048]{2,1,0:T(8,128)(2,1)}, bf16[16,16,2048]{2,1,0:T(8,128)(2,1)S(1)}, u32[]{:S(2)}) copy-start(bf16[16,16,2048]{2,1,0:T(8,128)(2,1)S(1)} %get-tuple-element.8) | copy-start | bytes 3145732
  117.8 4.6 %copy-start = (bf16[256,2048]{1,0:T(8,128)(2,1)S(1)}, bf16[256,2048]{1,0:T(8,128)(2,1)}, u32[]{:S(2)}) copy-start(bf16[256,2048]{1,0:T(8,128)(2,1)} %fusion.45) | copy-start | bytes 3145732
  117.9 4.9 %copy-start.1 = (bf16[256,2048]{1,0:T(8,128)(2,1)S(1)}, bf16[256,2048]{1,0:T(8,128)(2,1)}, u32[]{:S(2)}) copy-start(bf16[256,2048]{1,0:T(8,128)(2,1)} %fusion.39) | copy-start | bytes 3145732
  117.9 5.2 %copy-start.3 = (bf16[16,80,64]{1,2,0:T(8,128)(2,1)S(1)}, bf16[16,80,64]{1,2,0:T(8,128)(2,1)}, u32[]{:S(2)}) copy-start(bf16[16,80,64]{1,2,0:T(8,128)(2,1)} %get-tuple-element.10) | copy-start | bytes 491524
  117.9 5.2 %copy-start.4 = (bf16[16,80,64]{1,2,0:T(8,128)(2,1)S(1)}, bf16[16,80,64]{1,2,0:T(8,128)(2,1)}, u32[]{:S(2)}) copy-start(bf16[16,80,64]{1,2,0:T(8,128)(2,1)} %get-tuple-element.11) | copy-start | bytes 491524
Sparse Core Ops, SparseCore 0:
  9.5 53.2 all-gather.3
  129.4 102.0 reduce-scatter.1

commit v2 on v0

v2 whole, which is shorter than its diff:
```python
import functools

import jax
import jax.numpy as jnp
from jax import lax
from jax.experimental import pallas as pl
from jax.experimental.pallas import tpu as pltpu
from jax.sharding import PartitionSpec as P

F32, BF16 = jnp.float32, jnp.bfloat16
RELS = (0, 1, 7, 2, 6, 3, 5, 4)
SLOT = {r: i for i, r in enumerate(RELS)}
R, L = 0, 1


def _kernel(nch, ch, cap, nz, x_hbm, meta_ref, w1, w3, w2, out_ref,
            X, M, W, XG, U, OH, GT, OWN, SIB, S, RR,
            xs, wsem, ags, agr, ms, mr, ss, sr, ds_, dr, rs, rr):
    T, D = x_hbm.shape
    el, F = w1.shape[0], w1.shape[2]
    DC = D // nch
    HC = DC // 2
    KH = D // 2
    NT = min(256, F)
    k = meta_ref.shape[0] // 2
    caps = [ch] + [cap] * (el - 1)
    offs = [2 * sum(caps[:i]) for i in range(el)]
    rows = 2 * sum(caps)

    idx = lax.axis_index('expert')
    core = idx % 2
    chip = idx // 2
    cz, cy = chip // 2, chip % 2
    pos = cz * (1 - cy) + (2 * nz - 1 - cz) * cy

    def device(p):
        y = p // nz
        z = p * (1 - y) + (2 * nz - 1 - p) * y
        return (z * 2 + y) * 2 + core

    right = device((pos + 1) % (2 * nz))
    left = device((pos + 2 * nz - 1) % (2 * nz))
    side = chip * 2 + 1 - core
    dev = (right, left)

    def remote(src, dst, s_sem, r_sem, who):
        return pltpu.make_async_remote_copy(src_ref=src, dst_ref=dst, send_sem=s_sem, recv_sem=r_sem,
                                            device_id={'expert': who}, device_id_type=pl.DeviceIdType.MESH)

    wloads = []
    for e in range(el):
        for j, w in enumerate((w1, w1, w3, w3)):
            wloads.append(pltpu.make_async_copy(w.at[e, pl.ds((j % 2) * KH, KH), :], W.at[4 * e + j], wsem.at[4 * e + j]))
    xloads = [pltpu.make_async_copy(x_hbm.at[:, pl.ds(c * DC, DC)], X.at[c, pl.ds(0, T), :], xs.at[c]) for c in range(nch)]
    for c in xloads:
        c.start()
    for c in wloads:
        c.start()
    M[0] = meta_ref[...]

    barrier = pltpu.get_barrier_semaphore()
    for who in (right, left, side):
        pl.semaphore_signal(barrier, inc=1, device_id={'expert': who}, device_id_type=pl.DeviceIdType.MESH)
    pl.semaphore_wait(barrier, 3)

    hc = nch // 2

    def blk(rel, s, hf):
        return X.at[pl.ds(hf * hc, hc), pl.ds(SLOT[rel] * 2 * T + s * T, T), :]

    def has(d, s, hf):
        return s <= 3 or (s == 4 and hf == d)

    def ag(d, s, hf):
        a, b = ((1 - s) % 8, -s % 8) if d == R else (s - 1, s)
        return remote(blk(a, 0, hf), blk(b, 0, hf), ags.at[d, s - 1, hf], agr.at[d, s - 1, hf], dev[d])

    def hasm(d, s):
        return s <= 3 or (s == 4 and d == R)

    def agm(d, s):
        a, b = ((1 - s) % 8, -s % 8) if d == R else (s - 1, s)
        return remote(M.at[2 * SLOT[a]], M.at[2 * SLOT[b]], ms.at[d, s - 1], mr.at[d, s - 1], dev[d])

    def sd(rel, hf):
        return remote(blk(rel, 0, hf), blk(rel, 1, hf), ss.at[rel, hf], sr.at[rel, hf], side)

    def sdm(rel):
        return remote(M.at[2 * SLOT[rel]], M.at[2 * SLOT[rel] + 1], ss.at[rel, 2], sr.at[rel, 2], side)

    sent = []

    def go(c):
        c.start()
        sent.append(c)

    for c in xloads:
        c.wait()
    for d in (R, L):
        go(agm(d, 1))
    for hf in range(2):
        for d in (R, L):
            go(ag(d, 1, hf))
    go(sdm(0))
    for hf in range(2):
        go(sd(0, hf))

    def advance(s, hf):
        if hf == 0:
            for d in (R, L):
                if hasm(d, s):
                    agm(d, s).wait_recv()
                    if hasm(d, s + 1) and s < 4:
                        go(agm(d, s + 1))
                    go(sdm(-s % 8 if d == R else s))
        for d in (R, L):
            if has(d, s, hf):
                ag(d, s, hf).wait_recv()
                if s < 4 and has(d, s + 1, hf):
                    go(ag(d, s + 1, hf))
                go(sd(-s % 8 if d == R else s, hf))

    tr = lax.broadcasted_iota(jnp.int32, (2 * T, 2 * T), 0)
    tc = lax.broadcasted_iota(jnp.int32, (2 * T, 2 * T), 1)
    tri = jnp.where((tr < tc) & (tr // T == tc // T), 1.0, 0.0).astype(BF16)

    def prep(slot):
        m = M[2 * slot] + pltpu.roll(M[2 * slot + 1], T, 1)
        ids, gs = m[:k], m[k:]
        hits, gates = [], []
        for le in range(el):
            eq = ids == (idx * el + le).astype(F32)
            hits.append(jnp.max(jnp.where(eq, 1.0, 0.0), axis=0, keepdims=True))
            gates.append(jnp.sum(jnp.where(eq, gs, 0.0), axis=0, keepdims=True))
        hm = jnp.concatenate(hits + [jnp.zeros((16 - el, 2 * T), F32)], axis=0)
        rank = jnp.dot(hm.astype(BF16), tri, preferred_element_type=F32)
        lane = lax.broadcasted_iota(jnp.int32, (1, 2 * T), 1)
        oh, gg = [], []
        for le in range(el):
            key = jnp.where(hits[le] > 0.0, rank[le:le + 1] + jnp.where(lane >= T, float(caps[le]), 0.0), -1.0)
            hit = lax.broadcasted_iota(jnp.int32, (2 * caps[le], 2 * T), 0).astype(F32) == key
            oh.append(jnp.where(hit, 1.0, 0.0))
            gg.append(jnp.where(hit, gates[le], 0.0))
        OH[slot] = jnp.concatenate(oh, axis=0).astype(BF16)
        gv = jnp.concatenate(gg, axis=0)
        hi = gv.astype(BF16).astype(F32)
        mid = (gv - hi).astype(BF16).astype(F32)
        lo = gv - hi - mid
        GT[slot] = jnp.concatenate([hi, mid, lo], axis=0).T.astype(BF16)

    def arrive(g):
        for rel in RELS[4 * g:4 * g + 4]:
            for hf in range(2):
                sd(rel, hf).wait_recv()
            sdm(rel).wait_recv()

    def gather(g):
        def body(i, _):
            slot = 4 * g + i
            prep(slot)
            for c in range(nch):
                v = jnp.dot(OH[slot], X[c, pl.ds(pl.multiple_of(slot * 2 * T, 2 * T), 2 * T), :], preferred_element_type=F32).astype(BF16)
                for le in range(el):
                    n2 = 2 * caps[le]
                    XG[pl.ds(pl.multiple_of(4 * offs[le] + i * n2, 16), n2), c * DC:(c + 1) * DC] = v[offs[le]:offs[le] + n2]
            return 0
        lax.fori_loop(0, 4, body, 0)

    def expert(e, g):
        m = 8 * caps[e]
        src = pl.ds(4 * offs[e], m)
        dst = pl.ds(8 * offs[e] + g * m, m)

        def body(n, _):
            cols = pl.ds(pl.multiple_of(n * NT, NT), NT)
            xa, xb = XG[src, :KH], XG[src, KH:]
            a = jnp.dot(xa, W[4 * e, :, cols], preferred_element_type=F32) + jnp.dot(xb, W[4 * e + 1, :, cols], preferred_element_type=F32)
            b = jnp.dot(xa, W[4 * e + 2, :, cols], preferred_element_type=F32) + jnp.dot(xb, W[4 * e + 3, :, cols], preferred_element_type=F32)
            U[dst, cols] = (a * jax.nn.sigmoid(a) * b).astype(BF16)
            return 0
        lax.fori_loop(0, F // NT, body, 0)

    def loaded(e):
        for c in wloads[4 * e:4 * e + 4]:
            c.wait()

    for s in (1, 2):
        for hf in range(2):
            advance(s, hf)
    arrive(0)
    gather(0)
    loaded(0)
    expert(0, 0)
    advance(3, 0)
    loaded(1)
    expert(1, 0)
    advance(3, 1)
    loaded(2)
    expert(2, 0)
    loaded(3)
    expert(3, 0)
    advance(4, 0)
    advance(4, 1)
    arrive(1)
    gather(1)
    w2loads = []
    for e in range(el):
        expert(e, 1)
        if e < 2:
            for j in range(el):
                c = pltpu.make_async_copy(w2.at[j, :, pl.ds(e * KH, KH)], W.at[4 * e + j], wsem.at[4 * e + j])
                c.start()
                w2loads.append(c)
    for c in sent:
        c.wait_send()
    del sent[:]

    def h_rows(slot, lo, n):
        return X.at[slot // 2, pl.ds((slot % 2) * 3 * rows + lo, n), :]

    NF = 5

    def d2d(c, part):
        sl = pl.ds(NF, 8 - NF) if part == 0 else pl.ds(0, NF)
        return remote(SIB.at[c % 2, sl], S.at[c, sl], ds_.at[c, part], dr.at[c, part], side)

    def tile(c):
        hf, off = c // 2, (c % 2) * DC
        if off == 0:
            for w in w2loads[4 * hf:4 * hf + 4]:
                w.wait()
        if c >= 2:
            for part in range(2):
                d2d(c - 2, part).wait_send()
        nt = min(256, DC)
        for e in range(el):
            m = 16 * caps[e]
            n2 = 2 * caps[e]
            for n in range(DC // nt):
                h = jnp.dot(U[pl.ds(8 * offs[e], m), :], W[4 * hf + e, :, pl.ds(off + n * nt, nt)], preferred_element_type=F32).astype(BF16)
                for slot in range(8):
                    for p in range(3):
                        h_rows(slot, p * rows + offs[e], n2)[:, n * nt:(n + 1) * nt] = h[slot * n2:(slot + 1) * n2]
        for part in range(2):
            lo, hi = (NF, 8) if part == 0 else (0, NF)

            def body(slot, _):
                src = pl.ds(pl.multiple_of((slot % 2) * 3 * rows, 16), 3 * rows)
                v = jnp.dot(GT[slot], X[slot // 2, src, :], preferred_element_type=F32)
                OWN[c, slot] = v[:T]
                SIB[c % 2, slot] = v[T:]
                return 0
            lax.fori_loop(lo, hi, body, 0)
            d2d(c, part).start()

    A, B = slice(0, HC), slice(HC, DC)

    def ring(c, s, d):
        cols = pl.ds(0, DC) if s else pl.ds(d * HC, HC)
        rel = 4 - s if d == R else 4 + s
        return remote(OWN.at[c, SLOT[rel], :, cols], RR.at[c, d, s, :, cols], rs.at[c, d, s], rr.at[c, d, s], dev[d])

    def step(c, s):
        if s == 0:
            d2d(c, 0).wait_recv()
            OWN[c, SLOT[4]] += S[c, SLOT[4]]
        if s == 2:
            d2d(c, 1).wait_recv()
        for d in (R, L):
            if s:
                q = SLOT[4 - s if d == R else 4 + s]
                ring(c, s - 1, d).wait_recv()
                if s == 1:
                    h, o = (A, B) if d == R else (B, A)
                    OWN[c, q, :, h] += S[c, q, :, h] + RR[c, d, 0, :, h]
                    OWN[c, q, :, o] += S[c, q, :, o]
                else:
                    OWN[c, q] += S[c, q] + RR[c, d, s - 1]
            go(ring(c, s, d))

    def final(c):
        for d in (R, L):
            ring(c, 3, d).wait_recv()
        y = OWN[c, 0] + S[c, 0] + (RR[c, R, 3] + RR[c, L, 3])
        out_ref[:, c * DC:(c + 1) * DC] = y.astype(BF16)

    tile(0)
    tile(1)
    step(0, 0)
    tile(2)
    step(1, 0)
    step(0, 1)
    tile(3)
    step(2, 0)
    step(1, 1)
    step(0, 2)
    step(3, 0)
    step(2, 1)
    step(1, 2)
    step(0, 3)
    step(3, 1)
    step(2, 2)
    step(1, 3)
    final(0)
    step(3, 2)
    step(2, 3)
    final(1)
    step(3, 3)
    final(2)
    final(3)
    for c in sent:
        c.wait_send()
    for c in (2, 3):
        for part in range(2):
            d2d(c, part).wait_send()


def solution(mesh):
    n = mesh.shape['expert']
    nz = n // 4

    def local(x, idx, g, hot_tok, w1, w3, w2):
        t, d = x.shape
        k = idx.shape[1]
        el, _, f = w1.shape
        e = el * n
        ch = hot_tok.shape[0]
        cap = 2 * ((t * k - ch + e - 2) // (e - 1))
        nch = 4
        dc = d // nch
        rows = 2 * (ch + (el - 1) * cap)
        meta = jnp.concatenate([idx.astype(F32).T, g.T], axis=0)
        meta = jnp.pad(meta, ((0, 0), (0, t)))
        dma = pltpu.SemaphoreType.DMA
        vmem = pl.BlockSpec(memory_space=pltpu.VMEM)
        hbm = pl.BlockSpec(memory_space=pl.ANY)
        return pl.pallas_call(
            functools.partial(_kernel, nch, ch, cap, nz),
            name='moe',
            out_shape=jax.ShapeDtypeStruct((t, d), BF16),
            in_specs=[hbm, vmem, hbm, hbm, hbm],
            out_specs=vmem,
            scratch_shapes=[
                pltpu.VMEM((nch, 16 * t, dc), BF16),
                pltpu.VMEM((16, 2 * k, 2 * t), F32),
                pltpu.VMEM((4 * el, d // 2, f), BF16),
                pltpu.VMEM((4 * rows, d), BF16),
                pltpu.VMEM((8 * rows, f), BF16),
                pltpu.VMEM((8, rows, 2 * t), BF16),
                pltpu.VMEM((8, 2 * t, 3 * rows), BF16),
                pltpu.VMEM((nch, 8, t, dc), F32),
                pltpu.VMEM((2, 8, t, dc), F32),
                pltpu.VMEM((nch, 8, t, dc), F32),
                pltpu.VMEM((nch, 2, 4, t, dc), F32),
                dma((nch,)), dma((4 * el,)),
                dma((2, 4, 2)), dma((2, 4, 2)), dma((2, 4)), dma((2, 4)),
                dma((8, 3)), dma((8, 3)), dma((nch, 2)), dma((nch, 2)),
                dma((nch, 2, 4)), dma((nch, 2, 4)),
            ],
            compiler_params=pltpu.CompilerParams(collective_id=0, has_side_effects=True, vmem_limit_bytes=67043328),
        )(x, meta, w1, w3, w2)

    rows = P(('data', 'expert'))
    wspec = P('expert')
    return jax.shard_map(local, mesh=mesh, in_specs=(rows, rows, rows, rows, wspec, wspec, wspec), out_specs=rows, check_vma=False)
```

time: 343 us -> 109 us (0.32)
  the two profiles are of different devices: /device:TPU:13 before, /device:TPU:0 now
where the time goes in v2:
time: 109 us
  Pallas kernels  105 us (96%)
  other arithmetic  1.98 us (2%)
  local copies, waits for them, and re-layouts  1.67 us (2%)
    pallas_call x1, Pallas kernels, local(): pl.pallas_call(functools.partial(_kernel, nch, ch, cap, nz), name='moe',...  105 us

profile of v2, /device:TPU:0, one launch (start us, length us, event | category | flops | bytes accessed | tf_op | source)
XLA Modules:
  0.0 108.6 jit_solution(8372265025823733012)
XLA Ops:
  0.0 0.7 convert_bitcast_fusion
  0.7 1.3 %select_maximum_fusion.meta_ref = f32[16,128]{1,0:T(8,128)} fusion(f32[8,64]{1,0:T(8,128)} %bitcast.3, f32[8,64]{1,0:T(8,128)S(1)} %convert_bitcast_fusion), kind=kLoop, calls=%fused_computation | loop fusion | flops 8192 | bytes 12288 | tf_op jit(solution)/shard_map/concatenate | solution.py:332
  2.0 104.9 %moe.1 = bf16[64,2048]{1,0:T(8,128)(2,1)} custom-call(bf16[64,2048]{1,0:T(8,128)(2,1)} %x_hbm.1, f32[16,128]{1,0:T(8,128)} %select_maximum_fusion.meta_ref, bf16[4,2048,1024]{2,1,0:T(8,128)(2,1)} %w1.1, bf16[4,2048,1024]{2,1,0:T(8,128)(2,1)} %w3.1, bf16[4,1024,2048]{2,1,0:T(8,128)(2,1)} %w2.1), custom_call_target="tpu_custom_call" | custom-call | tf_op jit(solution)/shard_map/moe/pallas_call | solution.py:337
  106.9 1.7 %copy.8 = bf16[64,2048]{1,0:T(8,128)(2,1)} copy(bf16[64,2048]{1,0:T(8,128)(2,1)} %moe.1) | data formatting | bytes 524288

commit v3 on v2

v3 whole, which is shorter than its diff:
```python
import functools

import jax
import jax.numpy as jnp
from jax import lax
from jax.experimental import pallas as pl
from jax.experimental.pallas import tpu as pltpu
from jax.sharding import PartitionSpec as P

F32, BF16 = jnp.float32, jnp.bfloat16
RELS = (0, 1, 7, 2, 6, 3, 5, 4)
SLOT = {r: i for i, r in enumerate(RELS)}
R, L = 0, 1


def _kernel(nch, ch, cap, nz, x_hbm, ids_ref, g_ref, w1, w3, w2, out_ref,
            X, M, W, V, XG, U, OH, GT, OWN, SF, SN, S, RR,
            xs, wsem, vsem, ags, agr, ms, mr, ss, sr, ds_, dr, rs, rr):
    T, D = x_hbm.shape
    el, F = w1.shape[0], w1.shape[2]
    DC = D // nch
    HC = DC // 2
    KH = D // 2
    NT = min(256, F)
    k = ids_ref.shape[0]
    caps = [ch] + [cap] * (el - 1)
    offs = [2 * sum(caps[:i]) for i in range(el)]
    rows = 2 * sum(caps)

    idx = lax.axis_index('expert')
    core = idx % 2
    chip = idx // 2
    cz, cy = chip // 2, chip % 2
    pos = cz * (1 - cy) + (2 * nz - 1 - cz) * cy

    def device(p):
        y = p // nz
        z = p * (1 - y) + (2 * nz - 1 - p) * y
        return (z * 2 + y) * 2 + core

    right = device((pos + 1) % (2 * nz))
    left = device((pos + 2 * nz - 1) % (2 * nz))
    side = chip * 2 + 1 - core
    dev = (right, left)

    def remote(src, dst, s_sem, r_sem, who):
        return pltpu.make_async_remote_copy(src_ref=src, dst_ref=dst, send_sem=s_sem, recv_sem=r_sem,
                                            device_id={'expert': who}, device_id_type=pl.DeviceIdType.MESH)

    xloads = [pltpu.make_async_copy(x_hbm.at[:, pl.ds(c * DC, DC)], X.at[c, pl.ds(0, T), :], xs.at[c]) for c in range(nch)]
    for c in xloads:
        c.start()
    M[0, :k, :T] = ids_ref[...].astype(F32)
    M[0, k:, :T] = g_ref[...]
    M[0, :, T:] = jnp.zeros((2 * k, T), F32)

    barrier = pltpu.get_barrier_semaphore()
    for who in (right, left, side):
        pl.semaphore_signal(barrier, inc=1, device_id={'expert': who}, device_id_type=pl.DeviceIdType.MESH)
    wloads = []
    for e in range(el):
        for j, w in enumerate((w1, w1, w3, w3)):
            wloads.append(pltpu.make_async_copy(w.at[e, pl.ds((j % 2) * KH, KH), :], W.at[4 * e + j], wsem.at[4 * e + j]))
    vloads = [pltpu.make_async_copy(w2.at[e, :, pl.ds(0, DC)], V.at[e], vsem.at[0, e]) for e in range(el)]
    for c in wloads + vloads:
        c.start()
    pl.semaphore_wait(barrier, 3)

    def blk(rel, s, q):
        return X.at[q, pl.ds(SLOT[rel] * 2 * T + s * T, T), :]

    def relof(d, s):
        return -s % 8 if d == R else s

    def quarter(d, i):
        return i if d == R else nch - 1 - i

    def has(s, i):
        return s <= 3 or i < nch // 2

    def ag(d, s, i):
        q = quarter(d, i)
        return remote(blk(relof(d, s - 1), 0, q), blk(relof(d, s), 0, q), ags.at[d, s - 1, q], agr.at[d, s - 1, q], dev[d])

    def hasm(d, s):
        return s <= 3 or (s == 4 and d == R)

    def agm(d, s):
        return remote(M.at[2 * SLOT[relof(d, s - 1)]], M.at[2 * SLOT[relof(d, s)]], ms.at[d, s - 1], mr.at[d, s - 1], dev[d])

    def sd(rel, q):
        return remote(blk(rel, 0, q), blk(rel, 1, q), ss.at[rel, q], sr.at[rel, q], side)

    def sdm(rel):
        return remote(M.at[2 * SLOT[rel]], M.at[2 * SLOT[rel] + 1], ss.at[rel, nch], sr.at[rel, nch], side)

    sent = []

    def go(c):
        c.start()
        sent.append(c)

    for d in (R, L):
        go(agm(d, 1))
    go(sdm(0))
    for c in xloads:
        c.wait()
    for i in range(nch):
        for d in (R, L):
            go(ag(d, 1, i))
    for i in range(nch):
        go(sd(0, i))

    def advance_meta(s):
        for d in (R, L):
            if hasm(d, s):
                agm(d, s).wait_recv()
                if s < 4 and hasm(d, s + 1):
                    go(agm(d, s + 1))
                go(sdm(relof(d, s)))

    def advance(s, i):
        for d in (R, L):
            ag(d, s, i).wait_recv()
            if s < 4 and has(s + 1, i):
                go(ag(d, s + 1, i))
            go(sd(relof(d, s), quarter(d, i)))

    tr = lax.broadcasted_iota(jnp.int32, (2 * T, 2 * T), 0)
    tc = lax.broadcasted_iota(jnp.int32, (2 * T, 2 * T), 1)
    tri = jnp.where((tr < tc) & (tr // T == tc // T), 1.0, 0.0).astype(BF16)
    lane = lax.broadcasted_iota(jnp.int32, (1, 2 * T), 1)

    def prep(slot):
        m = M[2 * slot] + pltpu.roll(M[2 * slot + 1], T, 1)
        ids, gs = m[:k], m[k:]
        hits, gates = [], []
        for le in range(el):
            eq = ids == (idx * el + le).astype(F32)
            hits.append(jnp.max(jnp.where(eq, 1.0, 0.0), axis=0, keepdims=True))
            gates.append(jnp.sum(jnp.where(eq, gs, 0.0), axis=0, keepdims=True))
        hm = jnp.concatenate(hits + [jnp.zeros((16 - el, 2 * T), F32)], axis=0)
        rank = jnp.dot(hm.astype(BF16), tri, preferred_element_type=F32)
        oh, gg = [], []
        for le in range(el):
            key = jnp.where(hits[le] > 0.0, rank[le:le + 1] + jnp.where(lane >= T, float(caps[le]), 0.0), -1.0)
            hit = lax.broadcasted_iota(jnp.int32, (2 * caps[le], 2 * T), 0).astype(F32) == key
            oh.append(jnp.where(hit, 1.0, 0.0))
            gg.append(jnp.where(hit, gates[le], 0.0))
        OH[slot] = jnp.concatenate(oh, axis=0).astype(BF16)
        gv = jnp.concatenate(gg, axis=0)
        hi = gv.astype(BF16).astype(F32)
        mid = (gv - hi).astype(BF16).astype(F32)
        lo = gv - hi - mid
        GT[slot] = jnp.concatenate([hi, mid, lo], axis=0).T.astype(BF16)

    def preps(lo, n):
        for j in range(n):
            prep(lo + j)

    NEAR = 5
    passes = ((0, NEAR), (NEAR, 8))

    def arrive(g):
        for rel in RELS[passes[g][0]:passes[g][1]]:
            for q in range(nch):
                sd(rel, q).wait_recv()

    def gather(g):
        lo, hi = passes[g]
        nc = hi - lo
        for c in range(nch):
            for i in range(nc):
                v = jnp.dot(OH[lo + i], X[c, (lo + i) * 2 * T:(lo + i + 1) * 2 * T, :], preferred_element_type=F32).astype(BF16)
                for le in range(el):
                    n2 = 2 * caps[le]
                    r0 = nc * offs[le] + i * n2
                    XG[r0:r0 + n2, c * DC:(c + 1) * DC] = v[offs[le]:offs[le] + n2]

    def experts(g, n):
        lo, hi = passes[g]
        nc = hi - lo
        cols = pl.ds(pl.multiple_of(n * NT, NT), NT)
        for e in range(el):
            m = nc * 2 * caps[e]
            src = pl.ds(nc * offs[e], m)
            dst = pl.ds(8 * offs[e] + lo * 2 * caps[e], m)
            xa, xb = XG[src, :KH], XG[src, KH:]
            a = jnp.dot(xa, W[4 * e, :, cols], preferred_element_type=F32) + jnp.dot(xb, W[4 * e + 1, :, cols], preferred_element_type=F32)
            b = jnp.dot(xa, W[4 * e + 2, :, cols], preferred_element_type=F32) + jnp.dot(xb, W[4 * e + 3, :, cols], preferred_element_type=F32)
            U[dst, cols] = (a * jax.nn.sigmoid(a) * b).astype(BF16)

    steps = F // NT

    advance_meta(1)
    advance_meta(2)
    advance(1, 0)
    advance_meta(3)
    advance(1, 1)
    advance_meta(4)
    advance(1, 2)
    for rel in RELS:
        sdm(rel).wait_recv()
    preps(0, 2)
    advance(1, 3)
    preps(2, 2)
    advance(2, 0)
    preps(4, 2)
    advance(2, 1)
    preps(6, 2)
    advance(2, 2)
    advance(2, 3)
    arrive(0)
    gather(0)
    advance(3, 0)
    for c in wloads:
        c.wait()
    for n in range(steps):
        experts(0, n)
        for i in ((1, 2), (3,), (), ())[n % 4] if steps == 4 else (1, 2, 3):
            advance(3, i)
    advance(4, 0)
    advance(4, 1)
    arrive(1)
    gather(1)

    def far(n, _):
        experts(1, n)
        return 0
    lax.fori_loop(0, steps, far, 0)
    w2loads = []
    for c in range(1, nch):
        for e in range(el):
            w2loads.append(pltpu.make_async_copy(w2.at[e, :, pl.ds(c * DC, DC)], W.at[4 * (c // 2) + e, :, pl.ds((c % 2) * DC, DC)], vsem.at[c, e]))
            w2loads[-1].start()
    for c in sent:
        c.wait_send()
    del sent[:]

    def h_rows(slot, lo, n):
        return X.at[slot // 2, pl.ds((slot % 2) * 3 * rows + lo, n), :]

    def d2d(c, part):
        if part == 0:
            return remote(SF.at[c], S.at[c, pl.ds(NEAR, 8 - NEAR)], ds_.at[c, 0], dr.at[c, 0], side)
        return remote(SN.at[c % 2], S.at[c, pl.ds(0, NEAR)], ds_.at[c, 1], dr.at[c, 1], side)

    nt = min(256, DC)

    def tile(c, part):
        lo, hi = passes[1 - part]
        if part == 0:
            for w in vloads if c == 0 else w2loads[4 * c - 4:4 * c]:
                w.wait()
        elif c >= 2:
            d2d(c - 2, 1).wait_send()
        for e in range(el):
            n2 = 2 * caps[e]
            m = (hi - lo) * n2
            for n in range(DC // nt):
                if c == 0:
                    w = V[e, :, n * nt:(n + 1) * nt]
                else:
                    w = W[4 * (c // 2) + e, :, pl.ds((c % 2) * DC + n * nt, nt)]
                h = jnp.dot(U[pl.ds(8 * offs[e] + lo * n2, m), :], w, preferred_element_type=F32).astype(BF16)
                for j in range(hi - lo):
                    for p in range(3):
                        h_rows(lo + j, p * rows + offs[e], n2)[:, n * nt:(n + 1) * nt] = h[j * n2:(j + 1) * n2]
        for slot in range(lo, hi):
            v = jnp.dot(GT[slot], h_rows(slot, 0, 3 * rows)[...], preferred_element_type=F32)
            OWN[c, slot] = v[:T]
            if part == 0:
                SF[c, slot - NEAR] = v[T:]
            else:
                SN[c % 2, slot] = v[T:]
        d2d(c, part).start()

    A, B = slice(0, HC), slice(HC, DC)

    def ring(c, s, d):
        cols = pl.ds(0, DC) if s else pl.ds(d * HC, HC)
        rel = 4 - s if d == R else 4 + s
        return remote(OWN.at[c, SLOT[rel], :, cols], RR.at[c, d, s, :, cols], rs.at[c, d, s], rr.at[c, d, s], dev[d])

    def step(c, s):
        if s == 0:
            d2d(c, 0).wait_recv()
            OWN[c, SLOT[4]] += S[c, SLOT[4]]
        if s == 2:
            d2d(c, 1).wait_recv()
        for d in (R, L):
            if s:
                q = SLOT[4 - s if d == R else 4 + s]
                ring(c, s - 1, d).wait_recv()
                if s == 1:
                    h, o = (A, B) if d == R else (B, A)
                    OWN[c, q, :, h] += S[c, q, :, h] + RR[c, d, 0, :, h]
                    OWN[c, q, :, o] += S[c, q, :, o]
                else:
                    OWN[c, q] += S[c, q] + RR[c, d, s - 1]
            go(ring(c, s, d))

    def final(c):
        for d in (R, L):
            ring(c, 3, d).wait_recv()
        y = OWN[c, 0] + S[c, 0] + (RR[c, R, 3] + RR[c, L, 3])
        out_ref[:, c * DC:(c + 1) * DC] = y.astype(BF16)

    tile(0, 0)
    for c in range(1, nch):
        tile(c, 0)
        step(c - 1, 0)
    step(nch - 1, 0)
    for c in range(nch):
        step(c, 1)
        tile(c, 1)
    for s in (2, 3):
        for c in range(nch):
            step(c, s)
    for c in range(nch):
        final(c)
    for c in sent:
        c.wait_send()
    for c in range(nch):
        d2d(c, 0).wait_send()
    for c in (nch - 2, nch - 1):
        d2d(c, 1).wait_send()


def solution(mesh):
    n = mesh.shape['expert']
    nz = n // 4

    def local(x, idx, g, hot_tok, w1, w3, w2):
        t, d = x.shape
        k = idx.shape[1]
        el, _, f = w1.shape
        e = el * n
        ch = hot_tok.shape[0]
        cap = 2 * ((t * k - ch + e - 2) // (e - 1))
        nch = 4
        dc = d // nch
        rows = 2 * (ch + (el - 1) * cap)
        dma = pltpu.SemaphoreType.DMA
        vmem = pl.BlockSpec(memory_space=pltpu.VMEM)
        hbm = pl.BlockSpec(memory_space=pl.ANY)
        return pl.pallas_call(
            functools.partial(_kernel, nch, ch, cap, nz),
            name='moe',
            out_shape=jax.ShapeDtypeStruct((t, d), BF16),
            in_specs=[hbm, vmem, vmem, hbm, hbm, hbm],
            out_specs=vmem,
            scratch_shapes=[
                pltpu.VMEM((nch, 16 * t, dc), BF16),
                pltpu.VMEM((16, 2 * k, 2 * t), F32),
                pltpu.VMEM((4 * el, d // 2, f), BF16),
                pltpu.VMEM((el, f, dc), BF16),
                pltpu.VMEM((5 * rows, d), BF16),
                pltpu.VMEM((8 * rows, f), BF16),
                pltpu.VMEM((8, rows, 2 * t), BF16),
                pltpu.VMEM((8, 2 * t, 3 * rows), BF16),
                pltpu.VMEM((nch, 8, t, dc), F32),
                pltpu.VMEM((nch, 3, t, dc), F32),
                pltpu.VMEM((2, 5, t, dc), F32),
                pltpu.VMEM((nch, 8, t, dc), F32),
                pltpu.VMEM((nch, 2, 4, t, dc), F32),
                dma((nch,)), dma((4 * el,)), dma((nch, el)),
                dma((2, 4, nch)), dma((2, 4, nch)), dma((2, 4)), dma((2, 4)),
                dma((8, nch + 1)), dma((8, nch + 1)), dma((nch, 2)), dma((nch, 2)),
                dma((nch, 2, 4)), dma((nch, 2, 4)),
            ],
            compiler_params=pltpu.CompilerParams(collective_id=0, has_side_effects=True, vmem_limit_bytes=67043328),
        )(x, idx.T, g.T, w1, w3, w2)

    rows = P(('data', 'expert'))
    wspec = P('expert')
    return jax.shard_map(local, mesh=mesh, in_specs=(rows, rows, rows, rows, wspec, wspec, wspec), out_specs=rows, check_vma=False)
```

time: 109 us -> 91 us (0.83)
  Pallas kernels: 105 us -> 89.1 us
  other arithmetic: 1.98 us -> 0 us
    pallas_call x1, Pallas kernels: 105 us -> 89.1 us  [local(): pl.pallas_call(functools.partial(_kernel, nch, ch, cap, nz), name='moe',...]
    concatenate x1 -> x0, other arithmetic: 1.29 us -> none  [local(): meta = jnp.concatenate([idx.astype(F32).T, g.T], axis=0)]
where the time goes in v3:
time: 91 us; the launch traced here: 90.8 us
  Pallas kernels  89.1 us (98%)
  local copies, waits for them, and re-layouts  1.67 us (2%)
    pallas_call x1, Pallas kernels, local(): pl.pallas_call(functools.partial(_kernel, nch, ch, cap, nz), name='moe',...  89.1 us

profile of v3, /device:TPU:0, one launch (start us, length us, event | category | flops | bytes accessed | tf_op | source)
XLA Modules:
  0.0 90.8 jit_solution(567537122037272874)
XLA Ops:
  0.0 89.1 %moe.1 = bf16[64,2048]{1,0:T(8,128)(2,1)} custom-call(bf16[64,2048]{1,0:T(8,128)(2,1)} %x_hbm.1, s32[8,64]{1,0:T(8,128)} %bitcast.2, f32[8,64]{1,0:T(8,128)} %bitcast.3, bf16[4,2048,1024]{2,1,0:T(8,128)(2,1)} %w1.1, bf16[4,2048,1024]{2,1,0:T(8,128)(2,1)} %w3.1, bf16[4,1024,2048]{2,1,0:T(8,128)(2,1)} %w2.1), custom_call_target="tpu_custom_call" | custom-call | tf_op jit(solution)/shard_map/moe/pallas_call | solution.py:347
  89.1 1.7 %copy.8 = bf16[64,2048]{1,0:T(8,128)(2,1)} copy(bf16[64,2048]{1,0:T(8,128)(2,1)} %moe.1) | data formatting | bytes 524288

commit v4 on v3

--- a/solution.py
+++ b/solution.py
@@ -50,9 +50,8 @@
     xloads = [pltpu.make_async_copy(x_hbm.at[:, pl.ds(c * DC, DC)], X.at[c, pl.ds(0, T), :], xs.at[c]) for c in range(nch)]
     for c in xloads:
         c.start()
-    M[0, :k, :T] = ids_ref[...].astype(F32)
-    M[0, k:, :T] = g_ref[...]
-    M[0, :, T:] = jnp.zeros((2 * k, T), F32)
+    M[0, :, :T] = ids_ref[...].astype(F32)
+    M[0, :, T:] = g_ref[...]
 
     barrier = pltpu.get_barrier_semaphore()
     for who in (right, left, side):
@@ -132,8 +131,9 @@
     lane = lax.broadcasted_iota(jnp.int32, (1, 2 * T), 1)
 
     def prep(slot):
-        m = M[2 * slot] + pltpu.roll(M[2 * slot + 1], T, 1)
-        ids, gs = m[:k], m[k:]
+        mo, mi = M[2 * slot], M[2 * slot + 1]
+        ids = jnp.where(lane < T, mo, pltpu.roll(mi, T, 1))
+        gs = jnp.where(lane < T, pltpu.roll(mo, T, 1), mi)
         hits, gates = [], []
         for le in range(el):
             eq = ids == (idx * el + le).astype(F32)
@@ -154,27 +154,27 @@
         lo = gv - hi - mid
         GT[slot] = jnp.concatenate([hi, mid, lo], axis=0).T.astype(BF16)
 
-    def preps(lo, n):
-        for j in range(n):
-            prep(lo + j)
+    def tables(*slots):
+        for j in slots:
+            sdm(RELS[j]).wait_recv()
+        for j in slots:
+            prep(j)
 
     NEAR = 5
     passes = ((0, NEAR), (NEAR, 8))
 
-    def arrive(g):
-        for rel in RELS[passes[g][0]:passes[g][1]]:
+    def gather(g, lo, hi):
+        first, last = passes[g]
+        nc = last - first
+        for rel in RELS[lo:hi]:
             for q in range(nch):
                 sd(rel, q).wait_recv()
-
-    def gather(g):
-        lo, hi = passes[g]
-        nc = hi - lo
         for c in range(nch):
-            for i in range(nc):
-                v = jnp.dot(OH[lo + i], X[c, (lo + i) * 2 * T:(lo + i + 1) * 2 * T, :], preferred_element_type=F32).astype(BF16)
+            for i in range(lo, hi):
+                v = jnp.dot(OH[i], X[c, i * 2 * T:(i + 1) * 2 * T, :], preferred_element_type=F32).astype(BF16)
                 for le in range(el):
                     n2 = 2 * caps[le]
-                    r0 = nc * offs[le] + i * n2
+                    r0 = nc * offs[le] + (i - first) * n2
                     XG[r0:r0 + n2, c * DC:(c + 1) * DC] = v[offs[le]:offs[le] + n2]
 
     def experts(g, n):
@@ -192,42 +192,47 @@
 
     steps = F // NT
 
+    tables(0)
     advance_meta(1)
+    advance(1, 0)
+    advance(1, 1)
+    tables(1)
+    advance(1, 2)
+    tables(2)
+    advance(1, 3)
     advance_meta(2)
-    advance(1, 0)
+    advance(2, 0)
+    advance(2, 1)
+    tables(3)
+    advance(2, 2)
+    tables(4)
+    advance(2, 3)
     advance_meta(3)
-    advance(1, 1)
-    advance_meta(4)
-    advance(1, 2)
-    for rel in RELS:
-        sdm(rel).wait_recv()
-    preps(0, 2)
-    advance(1, 3)
-    preps(2, 2)
-    advance(2, 0)
-    preps(4, 2)
-    advance(2, 1)
-    preps(6, 2)
-    advance(2, 2)
-    advance(2, 3)
-    arrive(0)
-    gather(0)
+    gather(0, 0, NEAR)
     advance(3, 0)
     for c in wloads:
         c.wait()
+
+    def near(n):
+        if n < steps:
+            experts(0, n)
+
+    near(0)
+    advance(3, 1)
+    advance(3, 2)
+    tables(5, 6)
+    near(1)
+    advance(3, 3)
+    advance_meta(4)
+    near(2)
+    advance(4, 0)
+    tables(7)
+    near(3)
+    advance(4, 1)
+    gather(1, NEAR, 7)
+    gather(1, 7, 8)
     for n in range(steps):
-        experts(0, n)
-        for i in ((1, 2), (3,), (), ())[n % 4] if steps == 4 else (1, 2, 3):
-            advance(3, i)
-    advance(4, 0)
-    advance(4, 1)
-    arrive(1)
-    gather(1)
-
-    def far(n, _):
         experts(1, n)
-        return 0
-    lax.fori_loop(0, steps, far, 0)
     w2loads = []
     for c in range(1, nch):
         for e in range(el):
@@ -352,7 +357,7 @@
             out_specs=vmem,
             scratch_shapes=[
                 pltpu.VMEM((nch, 16 * t, dc), BF16),
-                pltpu.VMEM((16, 2 * k, 2 * t), F32),
+                pltpu.VMEM((16, k, 2 * t), F32),
                 pltpu.VMEM((4 * el, d // 2, f), BF16),
                 pltpu.VMEM((el, f, dc), BF16),
                 pltpu.VMEM((5 * rows, d), BF16),

time: 91 us -> 86 us (0.945)
  Pallas kernels: 89.1 us -> 84.1 us
    pallas_call x1, Pallas kernels: 89.1 us -> 84.1 us  [local(): pl.pallas_call(functools.partial(_kernel, nch, ch, cap, nz), name='moe',...]
where the time goes in v4:
time: 86 us; the launch traced here: 85.8 us
  Pallas kernels  84.1 us (98%)
  local copies, waits for them, and re-layouts  1.67 us (2%)
    pallas_call x1, Pallas kernels, local(): pl.pallas_call(functools.partial(_kernel, nch, ch, cap, nz), name='moe',...  84.1 us

profile of v4, /device:TPU:0, one launch (start us, length us, event | category | flops | bytes accessed | tf_op | source)
XLA Modules:
  0.0 85.8 jit_solution(2680986206999063148)
XLA Ops:
  0.0 84.1 %moe.1 = bf16[64,2048]{1,0:T(8,128)(2,1)} custom-call(bf16[64,2048]{1,0:T(8,128)(2,1)} %x_hbm.1, s32[8,64]{1,0:T(8,128)} %bitcast.2, f32[8,64]{1,0:T(8,128)} %bitcast.3, bf16[4,2048,1024]{2,1,0:T(8,128)(2,1)} %w1.1, bf16[4,2048,1024]{2,1,0:T(8,128)(2,1)} %w3.1, bf16[4,1024,2048]{2,1,0:T(8,128)(2,1)} %w2.1), custom_call_target="tpu_custom_call" | custom-call | tf_op jit(solution)/shard_map/moe/pallas_call | solution.py:352
  84.1 1.7 %copy.8 = bf16[64,2048]{1,0:T(8,128)(2,1)} copy(bf16[64,2048]{1,0:T(8,128)(2,1)} %moe.1) | data formatting | bytes 524288

commit v5 on v4

--- a/solution.py
+++ b/solution.py
@@ -161,7 +161,8 @@
             prep(j)
 
     NEAR = 5
-    passes = ((0, NEAR), (NEAR, 8))
+    passes = ((0, 3), (3, NEAR), (NEAR, 8))
+    parts = ((NEAR, 8), (0, NEAR))
 
     def gather(g, lo, hi):
         first, last = passes[g]
@@ -175,7 +176,7 @@
                 for le in range(el):
                     n2 = 2 * caps[le]
                     r0 = nc * offs[le] + (i - first) * n2
-                    XG[r0:r0 + n2, c * DC:(c + 1) * DC] = v[offs[le]:offs[le] + n2]
+                    XG[g % 2, r0:r0 + n2, c * DC:(c + 1) * DC] = v[offs[le]:offs[le] + n2]
 
     def experts(g, n):
         lo, hi = passes[g]
@@ -185,12 +186,16 @@
             m = nc * 2 * caps[e]
             src = pl.ds(nc * offs[e], m)
             dst = pl.ds(8 * offs[e] + lo * 2 * caps[e], m)
-            xa, xb = XG[src, :KH], XG[src, KH:]
+            xa, xb = XG[g % 2, src, :KH], XG[g % 2, src, KH:]
             a = jnp.dot(xa, W[4 * e, :, cols], preferred_element_type=F32) + jnp.dot(xb, W[4 * e + 1, :, cols], preferred_element_type=F32)
             b = jnp.dot(xa, W[4 * e + 2, :, cols], preferred_element_type=F32) + jnp.dot(xb, W[4 * e + 3, :, cols], preferred_element_type=F32)
             U[dst, cols] = (a * jax.nn.sigmoid(a) * b).astype(BF16)
 
     steps = F // NT
+
+    def body(g, n):
+        if n < steps:
+            experts(g, n)
 
     tables(0)
     advance_meta(1)
@@ -202,37 +207,38 @@
     advance(1, 3)
     advance_meta(2)
     advance(2, 0)
+    gather(0, 0, 3)
+    for c in wloads:
+        c.wait()
+    body(0, 0)
     advance(2, 1)
+    advance(2, 2)
     tables(3)
-    advance(2, 2)
-    tables(4)
+    body(0, 1)
     advance(2, 3)
     advance_meta(3)
-    gather(0, 0, NEAR)
+    tables(4)
+    body(0, 2)
     advance(3, 0)
-    for c in wloads:
-        c.wait()
-
-    def near(n):
-        if n < steps:
-            experts(0, n)
-
-    near(0)
+    body(0, 3)
     advance(3, 1)
+    gather(1, 3, NEAR)
+    body(1, 0)
     advance(3, 2)
-    tables(5, 6)
-    near(1)
+    tables(5)
+    body(1, 1)
     advance(3, 3)
     advance_meta(4)
-    near(2)
+    tables(6)
+    body(1, 2)
     advance(4, 0)
     tables(7)
-    near(3)
+    gather(2, NEAR, 7)
     advance(4, 1)
-    gather(1, NEAR, 7)
-    gather(1, 7, 8)
+    body(1, 3)
+    gather(2, 7, 8)
     for n in range(steps):
-        experts(1, n)
+        experts(2, n)
     w2loads = []
     for c in range(1, nch):
         for e in range(el):
@@ -253,7 +259,7 @@
     nt = min(256, DC)
 
     def tile(c, part):
-        lo, hi = passes[1 - part]
+        lo, hi = parts[part]
         if part == 0:
             for w in vloads if c == 0 else w2loads[4 * c - 4:4 * c]:
                 w.wait()
@@ -360,7 +366,7 @@
                 pltpu.VMEM((16, k, 2 * t), F32),
                 pltpu.VMEM((4 * el, d // 2, f), BF16),
                 pltpu.VMEM((el, f, dc), BF16),
-                pltpu.VMEM((5 * rows, d), BF16),
+                pltpu.VMEM((2, 3 * rows, d), BF16),
                 pltpu.VMEM((8 * rows, f), BF16),
                 pltpu.VMEM((8, rows, 2 * t), BF16),
                 pltpu.VMEM((8, 2 * t, 3 * rows), BF16),

time: 86 us -> 85.8 us (level)
  no operation moved by 1% of the time
where the time goes in v5:
time: 85.8 us; the launch traced here: 85.6 us
  Pallas kernels  83.9 us (98%)
  local copies, waits for them, and re-layouts  1.67 us (2%)
    pallas_call x1, Pallas kernels, local(): pl.pallas_call(functools.partial(_kernel, nch, ch, cap, nz), name='moe',...  83.9 us

profile of v5, /device:TPU:0, one launch (start us, length us, event | category | flops | bytes accessed | tf_op | source)
XLA Modules:
  0.0 85.6 jit_solution(16116916445016081144)
XLA Ops:
  0.0 83.9 %moe.1 = bf16[64,2048]{1,0:T(8,128)(2,1)} custom-call(bf16[64,2048]{1,0:T(8,128)(2,1)} %x_hbm.1, s32[8,64]{1,0:T(8,128)} %bitcast.2, f32[8,64]{1,0:T(8,128)} %bitcast.3, bf16[4,2048,1024]{2,1,0:T(8,128)(2,1)} %w1.1, bf16[4,2048,1024]{2,1,0:T(8,128)(2,1)} %w3.1, bf16[4,1024,2048]{2,1,0:T(8,128)(2,1)} %w2.1), custom_call_target="tpu_custom_call" | custom-call | tf_op jit(solution)/shard_map/moe/pallas_call | solution.py:358
  84.0 1.7 %copy.8 = bf16[64,2048]{1,0:T(8,128)(2,1)} copy(bf16[64,2048]{1,0:T(8,128)(2,1)} %moe.1) | data formatting | bytes 524288

commit v6 on v5

--- a/solution.py
+++ b/solution.py
@@ -47,15 +47,15 @@
         return pltpu.make_async_remote_copy(src_ref=src, dst_ref=dst, send_sem=s_sem, recv_sem=r_sem,
                                             device_id={'expert': who}, device_id_type=pl.DeviceIdType.MESH)
 
+    barrier = pltpu.get_barrier_semaphore()
+    for who in (right, left, side):
+        pl.semaphore_signal(barrier, inc=1, device_id={'expert': who}, device_id_type=pl.DeviceIdType.MESH)
     xloads = [pltpu.make_async_copy(x_hbm.at[:, pl.ds(c * DC, DC)], X.at[c, pl.ds(0, T), :], xs.at[c]) for c in range(nch)]
     for c in xloads:
         c.start()
     M[0, :, :T] = ids_ref[...].astype(F32)
     M[0, :, T:] = g_ref[...]
 
-    barrier = pltpu.get_barrier_semaphore()
-    for who in (right, left, side):
-        pl.semaphore_signal(barrier, inc=1, device_id={'expert': who}, device_id_type=pl.DeviceIdType.MESH)
     wloads = []
     for e in range(el):
         for j, w in enumerate((w1, w1, w3, w3)):

time: 85.8 us -> 95.2 us (1.11)
  Pallas kernels: 83.9 us -> 93.3 us
    pallas_call x1, Pallas kernels: 83.9 us -> 93.3 us  [local(): pl.pallas_call(functools.partial(_kernel, nch, ch, cap, nz), name='moe',...]
where the time goes in v6:
time: 95.2 us; the launch traced here: 95 us
  Pallas kernels  93.3 us (98%)
  local copies, waits for them, and re-layouts  1.67 us (2%)
    pallas_call x1, Pallas kernels, local(): pl.pallas_call(functools.partial(_kernel, nch, ch, cap, nz), name='moe',...  93.3 us

profile of v6, /device:TPU:0, one launch (start us, length us, event | category | flops | bytes accessed | tf_op | source)
XLA Modules:
  0.0 95.0 jit_solution(10267865684976230859)
XLA Ops:
  0.0 93.3 %moe.1 = bf16[64,2048]{1,0:T(8,128)(2,1)} custom-call(bf16[64,2048]{1,0:T(8,128)(2,1)} %x_hbm.1, s32[8,64]{1,0:T(8,128)} %bitcast.2, f32[8,64]{1,0:T(8,128)} %bitcast.3, bf16[4,2048,1024]{2,1,0:T(8,128)(2,1)} %w1.1, bf16[4,2048,1024]{2,1,0:T(8,128)(2,1)} %w3.1, bf16[4,1024,2048]{2,1,0:T(8,128)(2,1)} %w2.1), custom_call_target="tpu_custom_call" | custom-call | tf_op jit(solution)/shard_map/moe/pallas_call | solution.py:358
  93.3 1.7 %copy.8 = bf16[64,2048]{1,0:T(8,128)(2,1)} copy(bf16[64,2048]{1,0:T(8,128)(2,1)} %moe.1) | data formatting | bytes 524288
